TPU v7x, 128 devices: a whole 4x4x4 slice. The times are simulated.
128 devices in a mesh: expert: 16 (over z, x), tensor: 4 (over y), dp: 2 (over core).
Axes of the slice: x: 4, y: 4, z: 4, core: 2. Of those that a mesh axis runs over, the one named last changes fastest.
Arguments:
- tokens: bfloat16 [16384, 2048], P(('dp', 'expert', 'tensor')), parts along dimension 0, may hold values from -6 to 6
- expert_ids: int32 [16384, 4], P(('dp', 'expert', 'tensor')), parts along dimension 0, may hold values from 0 to 63, all different within a row; in each aligned block of 128 rows (0 to 127, 128 to 255, ...) at most 16 rows name the same one
- gate_probs: float32 [16384, 4], P(('dp', 'expert', 'tensor')), parts along dimension 0, may hold values from 0.05 to 0.6
- w_gate: bfloat16 [64, 2048, 1408], P(('expert', 'tensor')), may hold values from -0.125 to 0.125
- w_up: bfloat16 [64, 2048, 1408], P(('expert', 'tensor')), may hold values from -0.125 to 0.125
- w_down: bfloat16 [64, 1408, 2048], P(('expert', 'tensor')), may hold values from -0.15625 to 0.15625
- s_gate: bfloat16 [2048, 2816], P(None, 'tensor'), may hold values from -0.125 to 0.125
- s_up: bfloat16 [2048, 2816], P(None, 'tensor'), may hold values from -0.125 to 0.125
- s_down: bfloat16 [2816, 2048], P('tensor'), may hold values from -0.109375 to 0.109375
- shared_gate: bfloat16 [2048], replicated, may hold values from -0.125 to 0.125
Outputs:
- mixed: bfloat16 [16384, 2048], P(('dp', 'expert', 'tensor')), parts along dimension 0
There are 2 independent parts, one for each index of `dp`. A program takes and returns all parts, laid end to end along the dimension named above; an argument that names none is the same for every part. Nothing has to cross between parts.
Inputs may be any that keep to these rules, and one draw needn't show every extreme that they name: `expert_ids`: among the rows of one device, no expert is named by more than 16 of them.
All inputs are finite; a program needn't handle non-finite values.
Results may differ from a plain program's by a relative error of at most 0.0095.
Values may be sent and summed in bfloat16 or wider, within the bound.
No kernel may reach another device: no remote copies, remote signals or barrier semaphores. Data moves between devices by JAX's collectives and lax.ppermute only.
A program may use at most 128 MiB of HBM per device.

v0:
```python
import jax
import jax.numpy as jnp
from jax import lax
from jax.sharding import PartitionSpec as P


def split_up(x, dim, length):
    dims = x.shape
    pieces = x.reshape(*dims[:dim], length, dims[dim] // length, *dims[dim + 1 :])
    return jnp.moveaxis(pieces, dim, 0)


def in_order(pieces, dim):
    pieces = jnp.moveaxis(pieces, 0, dim)
    dims = pieces.shape
    return pieces.reshape(*dims[:dim], dims[dim] * dims[dim + 1], *dims[dim + 2 :])


def exchange_both(x, axis, axes, splits, concats):
    sizes = [lax.axis_size(a) for a in axes]
    pieces = split_up(x, splits[0], sizes[0])
    pieces = jnp.moveaxis(split_up(pieces, splits[1] + 1, sizes[1]), 0, 1)
    inside = pieces.shape[2:]
    pieces = pieces.reshape(-1, *inside)
    pieces = lax.all_to_all(pieces, axis, split_axis=0, concat_axis=0, tiled=True)
    pieces = in_order(pieces.reshape(*sizes, *inside), concats[0] + 1)
    return in_order(pieces, concats[1])


def sent_to_all(x, axis):
    length = lax.axis_size(axis)
    return lax.all_to_all(jnp.broadcast_to(x[None], (length, *x.shape)), axis, 0, 0, tiled=True)


def collect(x, axis, dim):
    return in_order(sent_to_all(x, axis), dim)


def summed_on_arrival(x, axis, dim):
    length = lax.axis_size(axis)
    pieces = lax.all_to_all(split_up(x, dim, length), axis, 0, 0, tiled=True)
    return jnp.sum(pieces.astype(jnp.float32), axis=0)


def silu_product(rows, w_first, w_second):
    gate = jnp.dot(rows, w_first, preferred_element_type=jnp.float32)
    up = jnp.dot(rows, w_second, preferred_element_type=jnp.float32)
    return (jax.nn.silu(gate) * up).astype(jnp.bfloat16)


def slot_index(ids, experts, capacity):
    flat = ids.reshape(-1)
    onehot = (flat[:, None] == jnp.arange(experts, dtype=jnp.int32)[None, :]).astype(jnp.int32)
    before = jnp.cumsum(onehot, axis=0) - onehot
    return flat * capacity + jnp.sum(before * onehot, axis=1)


def per_device(
    tokens, expert_ids, gate_probs, w_gate, w_up, w_down, s_gate, s_up, s_down, shared_gate
):
    tok_dev, width = tokens.shape
    top = expert_ids.shape[1]
    n_expert = lax.axis_size("expert")
    n_tensor = lax.axis_size("tensor")
    experts = n_expert * n_tensor
    capacity = max(2, 2 * top * tok_dev // experts)
    own_gate = w_gate[0]
    own_up = w_up[0]
    own_down = w_down[0]
    slot = slot_index(expert_ids, experts, capacity)
    repeated = jnp.repeat(tokens, top, axis=0)
    outgoing = jnp.zeros((experts * capacity, width), jnp.bfloat16).at[slot].set(repeated)
    outgoing = outgoing.reshape(experts, capacity, width)
    sectioned = outgoing.reshape(n_expert, n_tensor, capacity, width)
    arrived = exchange_both(sectioned, ("expert", "tensor"), ("expert", "tensor"), (0, 1), (0, 1))
    shape = arrived.shape
    flat_rows = arrived.reshape(-1, width)
    hidden = silu_product(flat_rows, own_gate, own_up)
    done = jnp.dot(hidden, own_down, preferred_element_type=jnp.float32).astype(jnp.bfloat16)
    finished = done.reshape(shape)
    back = exchange_both(finished, ("expert", "tensor"), ("expert", "tensor"), (0, 1), (0, 1))
    picked = back.reshape(experts * capacity, width)[slot].reshape(tok_dev, top, width)
    routed = jnp.einsum("tk,tkd->td", gate_probs, picked.astype(jnp.float32))
    shared_hidden = silu_product(collect(tokens, "tensor", 0), s_gate, s_up)
    shared = summed_on_arrival(
        jnp.dot(shared_hidden, s_down, preferred_element_type=jnp.float32).astype(jnp.bfloat16),
        "tensor",
        0,
    )
    scale = jax.nn.sigmoid(jnp.dot(tokens, shared_gate, preferred_element_type=jnp.float32))
    return (scale[:, None] * shared + routed).astype(jnp.bfloat16)


def solution(mesh):
    return jax.shard_map(
        per_device,
        mesh=mesh,
        in_specs=(
            P(("dp", "expert", "tensor"), None),
            P(("dp", "expert", "tensor"), None),
            P(("dp", "expert", "tensor"), None),
            P(("expert", "tensor"), None, None),
            P(("expert", "tensor"), None, None),
            P(("expert", "tensor"), None, None),
            P(None, "tensor"),
            P(None, "tensor"),
            P("tensor", None),
            P(),
        ),
        out_specs=P(("dp", "expert", "tensor"), None),
        check_vma=False,
    )
```

profile of v0, /device:TPU:4, one launch (start us, length us, event | category | flops | bytes accessed | tf_op | source)
XLA Modules:
  0.0 210.8 jit_solution(12412903686552456854)
XLA Ops:
  0.0 0.0 copy-start
  0.0 0.0 copy-start.4
  0.0 2.8 %broadcast_in_dim.6 = bf16[4,128,2048]{2,1,0:T(8,128)(2,1)} broadcast(bf16[128,2048]{1,0:T(8,128)(2,1)} %param.10), dimensions={1,2} | broadcast | bytes 2621440 | tf_op jit(solution)/shard_map/broadcast_in_dim | solution.py:32
  2.8 0.0 copy-start.2
  2.8 4.6 %all-to-all-start = ((bf16[4,128,2048]{2,1,0:T(8,128)(2,1)}), bf16[4,128,2048]{2,1,0:T(8,128)(2,1)}, u32[]{:S(2)}, u32[]{:S(2)}) async-start(bf16[4,128,2048]{2,1,0:T(8,128)(2,1)} %broadcast_in_dim.6), calls=%async_computation | async-start | bytes 4194304 | tf_op jit(solution)/shard_map/all_to_all | solution.py:32
  7.4 0.0 copy-done.4
  7.4 0.1 copy.16
  7.5 0.1 eq.29
  7.6 0.1 eq.25
  7.7 0.7 fusion.27
  8.4 2.4 %reduce-window.6 = s32[64,4,128]{2,0,1:T(8,128)S(1)} reduce-window(s32[64,4,128]{2,0,1:T(8,128)} %fusion.27, s32[]{:T(128)} %constant.11.clone.1), window={size=1x1x128 pad=0_0x0_0x127_0}, to_apply=%region_1.2 | reduce-window | flops 4161536 | bytes 262148 | tf_op jit(solution)/shard_map/reduce-window
  10.8 0.2 slice_reduce_fusion
  11.1 0.8 copy.15
  11.8 0.9 mul.47
  12.8 0.0 copy-done.2
  12.8 2.4 %broadcast_in_dim.8 = bf16[128,4,2048]{2,1,0:T(4,128)(2,1)} broadcast(bf16[128,2048]{1,0:T(8,128)(2,1)S(1)} %copy-done.2), dimensions={0,2} | broadcast | bytes 2621440 | tf_op jit(solution)/shard_map/broadcast_in_dim | solution.py:71
  15.2 4.0 %reshape.93 = bf16[512,2048]{1,0:T(8,128)(2,1)} reshape(bf16[128,4,2048]{2,1,0:T(4,128)(2,1)} %broadcast_in_dim.8) | data formatting | bytes 4194304 | tf_op jit(solution)/shard_map/reshape | solution.py:71
  19.2 0.1 fusion.26
  19.3 7.2 %scatter_custom_fusion = bf16[1024,2048]{1,0:T(8,128)(2,1)} fusion(s32[512]{0:T(512)S(1)} %bitcast.92, bf16[512,2048]{1,0:T(8,128)(2,1)} %reshape.93, bf16[]{:T(256)} %constant.5.clone.1), kind=kCustom, calls=%fused_computation.13 | custom fusion | bytes 4194816 | tf_op jit(solution)/shard_map/scatter | solution.py:72
  26.5 7.5 %all-to-all-done = bf16[4,128,2048]{2,1,0:T(8,128)(2,1)} async-done(((bf16[4,128,2048]{2,1,0:T(8,128)(2,1)}), bf16[4,128,2048]{2,1,0:T(8,128)(2,1)}, u32[]{:S(2)}, u32[]{:S(2)}) %all-to-all-start) | async-done | bytes 2097184 | tf_op jit(solution)/shard_map/all_to_all | solution.py:32
  34.0 9.6 %all-to-all-start.2 = ((bf16[64,1,1,16,2048]{4,3,2,1,0:T(8,128)(2,1)}), bf16[64,1,1,16,2048]{4,3,2,1,0:T(8,128)(2,1)}, u32[]{:S(2)}, u32[]{:S(2)}) async-start(bf16[64,1,1,16,2048]{4,3,2,1,0:T(8,128)(2,1)} %bitcast.88), calls=%async_computation.2 | async-start | bytes 8388608 | tf_op jit(solution)/shard_map/all_to_all | solution.py:25
  43.7 5.2 %fusion.30 = f32[512,704]{0,1:T(8,128)} fusion(bf16[512,2048]{1,0:T(8,128)(2,1)} %bitcast.1, bf16[2048,704]{0,1:T(8,128)(2,1)} %param.16), kind=kOutput, calls=%fused_computation.38 | convolution fusion | flops 1476395008 | bytes 6422528 | tf_op jit(solution)/shard_map/dot_general | solution.py:46
  48.9 0.0 copy-done
  48.9 7.6 %convolution_convert_fusion = bf16[512,2048]{1,0:T(8,128)(2,1)} fusion(bf16[704,2048]{1,0:T(8,128)(2,1)S(1)} %copy-done, bf16[512,2048]{1,0:T(8,128)(2,1)} %bitcast.1, bf16[2048,704]{0,1:T(8,128)(2,1)} %param.17, f32[512,704]{0,1:T(8,128)} %fusion.30), kind=kOutput, calls=%fused_computation.11 | convolution fusion | flops 2956001280 | bytes 11403264 | tf_op jit(solution)/shard_map/dot_general | solution.py:86
  56.6 40.1 %all-to-all-done.2 = bf16[64,1,1,16,2048]{4,3,2,1,0:T(8,128)(2,1)} async-done(((bf16[64,1,1,16,2048]{4,3,2,1,0:T(8,128)(2,1)}), bf16[64,1,1,16,2048]{4,3,2,1,0:T(8,128)(2,1)}, u32[]{:S(2)}, u32[]{:S(2)}) %all-to-all-start.2) | async-done | bytes 4194336 | tf_op jit(solution)/shard_map/all_to_all | solution.py:25
  96.7 3.6 %all-to-all-start.1 = ((bf16[4,128,2048]{2,1,0:T(8,128)(2,1)}), bf16[4,128,2048]{2,1,0:T(8,128)(2,1)S(1)}, u32[]{:S(2)}, u32[]{:S(2)}) async-start(bf16[4,128,2048]{2,1,0:T(8,128)(2,1)} %bitcast.90), calls=%async_computation.1 | async-start | bytes 4194304 | tf_op jit(solution)/shard_map/all_to_all | solution.py:41
  100.3 11.7 %fusion.4 = f32[1024,1408]{1,0:T(8,128)} fusion(bf16[1024,2048]{1,0:T(8,128)(2,1)} %bitcast.11, bf16[1,2048,1408]{2,1,0:T(8,128)(2,1)} %param.13), kind=kOutput, calls=%fused_computation.6 | convolution fusion | flops 5905580032 | bytes 15728640 | tf_op jit(solution)/shard_map/dot_general | solution.py:46
  112.0 20.6 %fusion.10 = bf16[1024,2048]{1,0:T(8,128)(2,1)} fusion(bf16[1,1408,2048]{2,1,0:T(8,128)(2,1)} %param.15, f32[1024,1408]{1,0:T(8,128)} %fusion.4, bf16[1024,2048]{1,0:T(8,128)(2,1)} %bitcast.11, bf16[1,2048,1408]{2,1,0:T(8,128)(2,1)} %param.14), kind=kOutput, calls=%fused_computation.10 | convolution fusion | flops 11821907968 | bytes 25690112 | tf_op jit(solution)/shard_map/dot_general | solution.py:79
  132.7 0.0 all-to-all-done.1
  132.7 0.0 copy-start.6
  132.7 0.0 copy-start.5
  132.7 8.6 %all-to-all-start.3 = ((bf16[64,1,1,16,2048]{4,3,2,1,0:T(8,128)(2,1)}), bf16[64,1,1,16,2048]{4,3,2,1,0:T(8,128)(2,1)}, u32[]{:S(2)}, u32[]{:S(2)}) async-start(bf16[64,1,1,16,2048]{4,3,2,1,0:T(8,128)(2,1)} %bitcast.89), calls=%async_computation.3 | async-start | bytes 8388608 | tf_op jit(solution)/shard_map/all_to_all | solution.py:25
  141.3 0.0 copy-done.6
  141.3 0.2 copy.20
  141.5 0.0 copy-done.5
  141.5 0.2 fusion.22
  141.8 1.4 convert_reduce_fusion
  143.2 51.2 %all-to-all-done.3 = bf16[64,1,1,16,2048]{4,3,2,1,0:T(8,128)(2,1)} async-done(((bf16[64,1,1,16,2048]{4,3,2,1,0:T(8,128)(2,1)}), bf16[64,1,1,16,2048]{4,3,2,1,0:T(8,128)(2,1)}, u32[]{:S(2)}, u32[]{:S(2)}) %all-to-all-start.3) | async-done | bytes 4194336 | tf_op jit(solution)/shard_map/all_to_all | solution.py:25
  194.4 8.0 %gather_fusion = bf16[512,2048]{1,0:T(8,128)(2,1)} fusion(bf16[1024,2048]{1,0:T(8,128)(2,1)} %bitcast.25, s32[1024]{0:T(1024)S(1)} %pad_clamp_fusion), kind=kCustom, calls=%fused_computation | custom fusion | bytes 4196352 | tf_op jit(solution)/shard_map/gather | solution.py:82
  202.4 0.0 copy-start.1
  202.4 4.3 %reshape.80 = bf16[128,4,2048]{2,1,0:T(4,128)(2,1)} reshape(bf16[512,2048]{1,0:T(8,128)(2,1)} %gather_fusion) | data formatting | bytes 4194304 | tf_op jit(solution)/shard_map/reshape | solution.py:82
  206.7 0.0 copy-start.3
  206.7 2.9 %fusion.31 = f32[128,1,2048]{2,1,0:T(1,128)S(1)} fusion(bf16[128,4,2048]{2,1,0:T(4,128)(2,1)} %reshape.80, bf16[128,4,1]{1,2,0:T(2,128)(2,1)S(1)} %copy.20), kind=kOutput, calls=%fused_computation.39 | convolution fusion | flops 2097152 | bytes 3146752 | tf_op jit(solution)/shard_map/tk,tkd->td/dot_general | solution.py:83
  209.6 0.0 copy-done.3
  209.6 1.2 fusion.23
  210.8 0.0 copy-done.1
  (6 shorter events, 0.1 us)
Async XLA Ops:
  0.0 48.9 %copy-start = (bf16[704,2048]{1,0:T(8,128)(2,1)S(1)}, bf16[704,2048]{1,0:T(8,128)(2,1)}, u32[]{:S(2)}) copy-start(bf16[704,2048]{1,0:T(8,128)(2,1)} %param.18) | copy-start | bytes 8650756
  0.0 7.4 %copy-start.4 = (s32[128,4]{0,1:T(4,128)S(1)}, s32[128,4]{0,1:T(4,128)}, u32[]{:S(2)}) copy-start(s32[128,4]{0,1:T(4,128)} %param.11) | copy-start | bytes 6148
  2.8 10.0 %copy-start.2 = (bf16[128,2048]{1,0:T(8,128)(2,1)S(1)}, bf16[128,2048]{1,0:T(8,128)(2,1)}, u32[]{:S(2)}) copy-start(bf16[128,2048]{1,0:T(8,128)(2,1)} %param.10) | copy-start | bytes 1572868
  2.8 31.2 %all-to-all-start = ((bf16[4,128,2048]{2,1,0:T(8,128)(2,1)}), bf16[4,128,2048]{2,1,0:T(8,128)(2,1)}, u32[]{:S(2)}, u32[]{:S(2)}) async-start(bf16[4,128,2048]{2,1,0:T(8,128)(2,1)} %broadcast_in_dim.6), calls=%async_computation | async-start | bytes 4194304 | tf_op jit(solution)/shard_map/all_to_all | solution.py:32
  34.0 62.6 %all-to-all-start.2 = ((bf16[64,1,1,16,2048]{4,3,2,1,0:T(8,128)(2,1)}), bf16[64,1,1,16,2048]{4,3,2,1,0:T(8,128)(2,1)}, u32[]{:S(2)}, u32[]{:S(2)}) async-start(bf16[64,1,1,16,2048]{4,3,2,1,0:T(8,128)(2,1)} %bitcast.88), calls=%async_computation.2 | async-start | bytes 8388608 | tf_op jit(solution)/shard_map/all_to_all | solution.py:25
  96.7 36.0 %all-to-all-start.1 = ((bf16[4,128,2048]{2,1,0:T(8,128)(2,1)}), bf16[4,128,2048]{2,1,0:T(8,128)(2,1)S(1)}, u32[]{:S(2)}, u32[]{:S(2)}) async-start(bf16[4,128,2048]{2,1,0:T(8,128)(2,1)} %bitcast.90), calls=%async_computation.1 | async-start | bytes 4194304 | tf_op jit(solution)/shard_map/all_to_all | solution.py:41
  132.7 8.7 %copy-start.6 = (f32[128,4]{0,1:T(4,128)S(1)}, f32[128,4]{0,1:T(4,128)}, u32[]{:S(2)}) copy-start(f32[128,4]{0,1:T(4,128)} %param.12) | copy-start | bytes 6148
  132.7 8.8 %copy-start.5 = (bf16[2048]{0:T(1024)(128)(2,1)S(1)}, bf16[2048]{0:T(1024)(128)(2,1)}, u32[]{:S(2)}) copy-start(bf16[2048]{0:T(1024)(128)(2,1)} %param.19) | copy-start | bytes 12292
  132.7 61.7 %all-to-all-start.3 = ((bf16[64,1,1,16,2048]{4,3,2,1,0:T(8,128)(2,1)}), bf16[64,1,1,16,2048]{4,3,2,1,0:T(8,128)(2,1)}, u32[]{:S(2)}, u32[]{:S(2)}) async-start(bf16[64,1,1,16,2048]{4,3,2,1,0:T(8,128)(2,1)} %bitcast.89), calls=%async_computation.3 | async-start | bytes 8388608 | tf_op jit(solution)/shard_map/all_to_all | solution.py:25
  202.4 8.4 %copy-start.1 = (bf16[704,2048]{1,0:T(8,128)(2,1)S(1)}, bf16[704,2048]{1,0:T(8,128)(2,1)}, u32[]{:S(2)}) copy-start(bf16[704,2048]{1,0:T(8,128)(2,1)} %param.18) | copy-start | bytes 8650756
  206.7 2.9 %copy-start.3 = (f32[128,2048]{1,0:T(8,128)S(1)}, f32[128,2048]{1,0:T(8,128)}, u32[]{:S(2)}) copy-start(f32[128,2048]{1,0:T(8,128)} %convert_reduce_fusion) | copy-start | bytes 3145732
where the time goes:
time: 212 us; the launch traced here: 211 us
  waiting for transfers between devices  98.9 us (47%)
  matrix products  48.4 us (23%)
  local copies, waits for them, and re-layouts  31.1 us (15%)
  starting transfers between devices  26.5 us (12%)
  other arithmetic  5.85 us (3%)
    all_to_all x2, waiting for transfers between devices, exchange_both(): lax.all_to_all(pieces, axis, split_axis=0, concat_axis=0, tiled=True)  91.3 us
    dot_general x1, matrix products, per_device(): jnp.dot(hidden, own_down, preferred_element_type=jnp.float32)  20.6 us
    all_to_all x2, starting transfers between devices, exchange_both(): lax.all_to_all(pieces, axis, split_axis=0, concat_axis=0, tiled=True)  18.3 us
    dot_general x2, matrix products, silu_product(): gate = jnp.dot(rows, w_first, preferred_element_type=jnp.float32)  17 us
    gather x1, local copies, waits for them, and re-layouts, per_device(): back.reshape(experts * capacity, width)[slot].reshape(tok_dev, top, width)  8 us
    dot_general x1, matrix products, per_device(): jnp.dot(shared_hidden, s_down, preferred_element_type=jnp.float32)  7.64 us
    all_to_all x1, waiting for transfers between devices, sent_to_all(): lax.all_to_all(jnp.broadcast_to(x[None], (length, *x.shape)), axis, 0, 0,...  7.54 us
    scatter x1, local copies, waits for them, and re-layouts, per_device(): jnp.zeros((experts * capacity, width), jnp.bfloat16).at[slot].set(repeated)  7.21 us
  transfers between devices with their start and end apart: 4, of which 3 were waited for; matrix products, arithmetic and copies ran while one was open for 31% of the time, Pallas kernels for 0%

commit v1 on v0

v1 whole, which is shorter than its diff:
```python
import functools

import jax
import jax.numpy as jnp
from jax import lax
from jax.experimental import pallas as pl
from jax.experimental.pallas import tpu as pltpu
from jax.sharding import PartitionSpec as P


BF16 = jnp.bfloat16
F32 = jnp.float32
VMEM = pl.BlockSpec(memory_space=pltpu.VMEM)
HBM = pl.BlockSpec(memory_space=pltpu.HBM)
LARGE = 60 * 1024 * 1024


def dot(a, b):
    return jnp.dot(a, b, preferred_element_type=F32)


def tdot(a, b):
    return lax.dot_general(a, b, (((0,), (0,)), ((), ())), preferred_element_type=F32)


def ndot(a, b):
    return lax.dot_general(a, b, (((1,), (1,)), ((), ())), preferred_element_type=F32)


def fetch(pairs, sems):
    copies = [pltpu.make_async_copy(a, b, sems.at[i]) for i, (a, b) in enumerate(pairs)]
    for c in copies:
        c.start()
    return copies


def finish(copies):
    for c in copies:
        c.wait()


def weigh(meta, shape, mine, members):
    groups, capacity, rows = shape
    top = meta.shape[0] // 2
    earlier = lax.broadcasted_iota(jnp.int32, (rows, rows), 0)
    later = lax.broadcasted_iota(jnp.int32, (rows, rows), 1)
    before = (earlier < later).astype(BF16)
    expert = lax.broadcasted_iota(jnp.int32, (groups, rows), 0).astype(F32) * members + mine
    place = lax.broadcasted_iota(jnp.int32, shape, 1).astype(F32)
    named = jnp.zeros((groups, rows), F32)
    prob = jnp.zeros((groups, rows), F32)
    for k in range(top):
        hit = meta[k : k + 1] == expert
        named = jnp.where(hit, 1.0, named)
        prob = jnp.where(hit, meta[top + k : top + k + 1], prob)
    rank = dot(named.astype(BF16), before)
    slot = jnp.where(named > 0.0, rank, -1.0)
    pick = slot[:, None, :] == place
    high = prob.astype(BF16).astype(F32)
    low = prob - high

    def spread(value):
        wide = jnp.where(pick, value, 0.0)
        return wide.reshape(groups * capacity, rows).astype(BF16)

    return spread(1.0), spread(high[:, None, :]), spread(low[:, None, :])


def route_kernel(count, groups, members, capacity, *refs):
    far, (out, high, low) = refs[: 2 * count], refs[2 * count : 2 * count + 3]
    near, sems = refs[2 * count + 3 : 4 * count + 3], refs[4 * count + 3]
    arrive = fetch(list(zip(far, near)), sems)
    mine = lax.axis_index("tensor").astype(F32)
    rows = high.shape[2]
    for i in range(count):
        arrive[i].wait()
        onehot, high[i], low[i] = weigh(near[i][...], (groups, capacity, rows), mine, members)
        arrive[count + i].wait()
        sent = dot(onehot, near[count + i][...]).astype(BF16)
        out[:, i * capacity : (i + 1) * capacity] = sent.reshape(groups, capacity, -1)


def route(metas, blocks, groups, members, capacity):
    count = len(blocks)
    rows, width = blocks[0].shape
    weights = jax.ShapeDtypeStruct((count, groups * capacity, rows), BF16)
    return pl.pallas_call(
        functools.partial(route_kernel, count, groups, members, capacity),
        out_shape=(
            jax.ShapeDtypeStruct((groups, count * capacity, width), BF16),
            weights,
            weights,
        ),
        in_specs=[HBM] * (2 * count),
        out_specs=(VMEM, VMEM, VMEM),
        scratch_shapes=[pltpu.VMEM(m.shape, F32) for m in metas]
        + [pltpu.VMEM(p.shape, BF16) for p in blocks]
        + [pltpu.SemaphoreType.DMA((2 * count,))],
        compiler_params=pltpu.CompilerParams(vmem_limit_bytes=LARGE),
        cost_estimate=pl.CostEstimate(
            flops=2 * count * groups * capacity * rows * width,
            bytes_accessed=count * (rows + groups * capacity) * width * 2,
            transcendentals=0,
        ),
        name="route",
    )(*metas, *blocks)


def pieces(total, size):
    starts = list(range(0, total - size + 1, size))
    ends = starts[1:] + [total]
    return list(zip(starts, ends))


AHEAD = 3


def mlp_kernel(fs, ns, block, turned, count, splits, *refs):
    xs, (wg, wu, wd) = refs[:count], refs[count : count + 3]
    outs, scratch = refs[count + 3 : count + 3 + splits], refs[count + 3 + splits :]
    x, vg, vu, vd, hidden, result, sems, x_sem = scratch
    total = x.shape[0]
    rows = total // count
    height = result.shape[1]
    copies = []
    for i, (a, b) in enumerate(fs):
        part = pl.ds(a, b - a) if turned else (slice(None), pl.ds(a, b - a))
        copies.append(
            (
                pltpu.make_async_copy(wg.at[part], vg.at[part], sems.at[0, i]),
                pltpu.make_async_copy(wu.at[part], vu.at[part], sems.at[1, i]),
            )
        )
    for i, (a, b) in enumerate(ns):
        part = (slice(None), pl.ds(a, b - a))
        copies.append((pltpu.make_async_copy(wd.at[part], vd.at[part], sems.at[2, i]),))

    def begin(i):
        if i < len(copies):
            for c in copies[i]:
                c.start()

    arrive = fetch([(xs[i], x.at[pl.ds(i * rows, rows)]) for i in range(count)], x_sem)
    for i in range(AHEAD):
        begin(i)
    finish(arrive)

    def over_rows(body):
        @pl.loop(0, total // block)
        def _(r):
            body(r, pl.ds(pl.multiple_of(r * block, block), block))

    for i, (a, b) in enumerate(fs):
        finish(copies[i])
        begin(i + AHEAD)

        def first(r, part):
            if turned:
                gate, up = ndot(x[part, :], vg[a:b, :]), ndot(x[part, :], vu[a:b, :])
            else:
                gate, up = dot(x[part, :], vg[:, a:b]), dot(x[part, :], vu[:, a:b])
            hidden[part, a:b] = (gate / (1.0 + jnp.exp(-gate)) * up).astype(BF16)

        over_rows(first)

    leave = []
    for i, (a, b) in enumerate(ns):
        finish(copies[len(fs) + i])
        begin(len(fs) + i + AHEAD)

        def second(r, part):
            value = dot(hidden[part, :], vd[:, a:b]).astype(BF16)
            several = block // height
            result[pl.ds(r * several, several), :, a:b] = value.reshape(several, height, b - a)

        over_rows(second)
        piece = height // splits
        for j in range(splits):
            leave.append(
                pltpu.make_async_copy(
                    result.at[:, pl.ds(j * piece, piece), pl.ds(a, b - a)],
                    outs[j].at[:, :, pl.ds(a, b - a)],
                    sems.at[j, i],
                )
            )
            leave[-1].start()
    finish(leave)


def mlp(xs, height, splits, wg, wu, wd, turned):
    width = xs[0].shape[1]
    total = sum(x.shape[0] for x in xs)
    inner = wd.shape[0]
    fs = pieces(inner, 256)
    ns = pieces(width, 512)
    out = jax.ShapeDtypeStruct((total // height, height // splits, width), BF16)
    return pl.pallas_call(
        functools.partial(mlp_kernel, fs, ns, 256, turned, len(xs), splits),
        out_shape=(out,) * splits,
        in_specs=[HBM] * (len(xs) + 3),
        out_specs=(HBM,) * splits,
        scratch_shapes=[
            pltpu.VMEM((total, width), BF16),
            pltpu.VMEM(wg.shape, BF16),
            pltpu.VMEM(wu.shape, BF16),
            pltpu.VMEM((inner, width), BF16),
            pltpu.VMEM((total, inner), BF16),
            pltpu.VMEM((total // height, height, width), BF16),
            pltpu.SemaphoreType.DMA((3, max(len(fs), len(ns)))),
            pltpu.SemaphoreType.DMA((len(xs),)),
        ],
        compiler_params=pltpu.CompilerParams(vmem_limit_bytes=LARGE),
        cost_estimate=pl.CostEstimate(
            flops=6 * total * width * inner,
            bytes_accessed=6 * width * inner + 4 * total * width,
            transcendentals=total * inner,
        ),
    )(*xs, wg, wu, wd)


def combine_kernel(order, final, *refs):
    count = len(order)
    inputs = 5 + count + final
    far, outs, scratch = refs[:inputs], refs[inputs : inputs + count], refs[inputs + count :]
    near, sems = scratch[:inputs], scratch[inputs]
    pairs = []
    for i in range(inputs):
        if i == 4:
            for j, d in enumerate(order):
                pairs.append((far[i].at[d], near[i].at[j]))
        else:
            pairs.append((far[i], near[i]))
    finish(fetch(pairs, sems))
    high, low, back, vector, shared = near[:5]
    tokens, others = near[5 : 5 + count], near[5 + count :]
    groups, height, width = back.shape
    capacity = height // count
    for i in range(count):
        logit = jnp.sum(
            tokens[i][...].astype(F32) * vector[...].astype(F32), axis=1, keepdims=True
        )
        scale = 1.0 / (1.0 + jnp.exp(-logit))
        part = back[:, i * capacity : (i + 1) * capacity].reshape(groups * capacity, width)
        total = tdot(high[i], part) + tdot(low[i], part) + scale * shared[i].astype(F32)
        for other in others:
            total = total + other[...].astype(F32)
        outs[i][...] = total.astype(BF16)


def combine(high, low, back, order, tokens, rows, vector, shared, others):
    count = len(order)
    width = back.shape[2]
    block = pltpu.VMEM((rows, width), BF16)
    return pl.pallas_call(
        functools.partial(combine_kernel, order, len(others)),
        out_shape=tuple(jax.ShapeDtypeStruct((rows, width), BF16) for _ in order),
        in_specs=[HBM] * (5 + count + len(others)),
        out_specs=tuple(VMEM for _ in order),
        scratch_shapes=[
            pltpu.VMEM(high.shape, BF16),
            pltpu.VMEM(low.shape, BF16),
            pltpu.VMEM(back.shape, BF16),
            pltpu.VMEM(vector.shape, BF16),
            pltpu.VMEM((count, rows, width), BF16),
        ]
        + [block] * (count + len(others))
        + [pltpu.SemaphoreType.DMA((4 + 2 * count + len(others),))],
        compiler_params=pltpu.CompilerParams(vmem_limit_bytes=LARGE),
        cost_estimate=pl.CostEstimate(
            flops=4 * back.size * rows // count,
            bytes_accessed=2 * back.size + 8 * count * rows * width,
            transcendentals=0,
        ),
    )(high, low, back, vector, shared, *tokens, *others)


def per_device(
    tokens, expert_ids, gate_probs, w_gate, w_up, w_down, s_gate, s_up, s_down, shared_gate
):
    rows, width = tokens.shape
    top = expert_ids.shape[1]
    groups = lax.axis_size("expert")
    members = lax.axis_size("tensor")
    capacity = max(2, 2 * top * rows // (groups * members))
    vector = shared_gate.reshape(1, width)

    def shift(x, d):
        return lax.ppermute(x, "tensor", [(i, (i + d) % members) for i in range(members)])

    def exchange(x):
        return lax.all_to_all(x, "expert", 0, 0, tiled=True)

    blocks, metas = {0: tokens}, {}
    metas[0] = jnp.concatenate([expert_ids.T.astype(F32), gate_probs.T], axis=0)
    for d in (1, 3, 2):
        blocks[d] = shift(tokens, -d)
        metas[d] = shift(metas[0], -d)

    def dispatch(chunk):
        sent, high, low = route(
            [metas[d] for d in chunk],
            [blocks[d] for d in chunk],
            groups,
            members,
            capacity,
        )
        return exchange(sent), high, low

    def expert(x, splits):
        flat = x.reshape(-1, width)
        return mlp([flat], x.shape[1], splits, w_gate[0], w_up[0], w_down[0], False)

    side, side_high, side_low = dispatch((1, 3))
    rest, rest_high, rest_low = dispatch((0, 2))
    shared = mlp(
        [blocks[d] for d in range(members)], rows, 1, s_gate.T, s_up.T, s_down, True
    )[0]
    (side,) = expert(side, 1)
    own, far = expert(rest, 2)
    back = exchange(side)
    first, third = combine(
        side_high,
        side_low,
        back,
        (1, 3),
        [blocks[1], blocks[3]],
        rows,
        vector,
        shared,
        [],
    )
    received = [shift(first, 1), shift(third, 3)]
    back = exchange(far)
    (second,) = combine(
        rest_high[1:], rest_low[1:], back, (2,), [blocks[2]], rows, vector, shared, []
    )
    received.append(shift(second, 2))
    back = exchange(own)
    return combine(
        rest_high[:1],
        rest_low[:1],
        back,
        (0,),
        [tokens],
        rows,
        vector,
        shared,
        received,
    )[0]


def solution(mesh):
    return jax.shard_map(
        per_device,
        mesh=mesh,
        in_specs=(
            P(("dp", "expert", "tensor"), None),
            P(("dp", "expert", "tensor"), None),
            P(("dp", "expert", "tensor"), None),
            P(("expert", "tensor"), None, None),
            P(("expert", "tensor"), None, None),
            P(("expert", "tensor"), None, None),
            P(None, "tensor"),
            P(None, "tensor"),
            P("tensor", None),
            P(),
        ),
        out_specs=P(("dp", "expert", "tensor"), None),
        check_vma=False,
    )
```

time: 212 us -> 202 us (0.953)
  Pallas kernels: 0 us -> 63.2 us
  matrix products: 48.4 us -> 0 us
  starting transfers between devices: 26.5 us -> 56.2 us
  waiting for transfers between devices: 98.9 us -> 72.2 us
  local copies, waits for them, and re-layouts: 31.1 us -> 7.55 us
  other arithmetic: 5.85 us -> 1.37 us
    pallas_call x0 -> x8, Pallas kernels: none -> 63.2 us  [the longest x3 45.8 us: mlp(): pl.pallas_call(functools.partial(mlp_kernel, fs, ns, 256, turned, len(xs)...]
    all_to_all x4 -> x5, waiting for transfers between devices: 98.9 us -> 39 us  [exchange(): return lax.all_to_all(x, 'expert', 0, 0, tiled=True)]
    dot_general x6 -> x0, matrix products: 48.4 us -> none  [the longest x1 20.6 us: per_device(): jnp.dot(hidden, own_down, preferred_element_type=jnp.float32)]
    ppermute x0 -> x9, waiting for transfers between devices: none -> 33.2 us  [shift(): lax.ppermute(x, 'tensor', [(i, (i + d) % members) for i in range(members)])]
    ppermute x0 -> x9, starting transfers between devices: none -> 16.6 us  [shift(): lax.ppermute(x, 'tensor', [(i, (i + d) % members) for i in range(members)])]
    all_to_all x4 -> x5, starting transfers between devices: 26.5 us -> 39.6 us  [exchange(): return lax.all_to_all(x, 'expert', 0, 0, tiled=True)]
    gather x1 -> x0, local copies, waits for them, and re-layouts: 8 us -> none  [per_device(): back.reshape(experts * capacity, width)[slot].reshape(tok_dev, top, width)]
    reshape x2 -> x1, local copies, waits for them, and re-layouts: 8.23 us -> 0.6 us  [per_device(): vector = shared_gate.reshape(1, width)]
  transfers between devices with their start and end apart: 4 -> 14, of which waited for: 3 -> 8; matrix products, arithmetic and copies ran while one was open for 31% -> 1% of each run, Pallas kernels for 0% -> 28%
where the time goes in v1:
time: 202 us; the launch traced here: 201 us
  waiting for transfers between devices  72.2 us (36%)
  Pallas kernels  63.2 us (31%)
  starting transfers between devices  56.2 us (28%)
  local copies, waits for them, and re-layouts  7.55 us (4%)
    pallas_call x3, Pallas kernels, mlp(): pl.pallas_call(functools.partial(mlp_kernel, fs, ns, 256, turned, len(xs)...  45.8 us
    all_to_all x5, starting transfers between devices, exchange(): return lax.all_to_all(x, 'expert', 0, 0, tiled=True)  39.6 us
    all_to_all x5, waiting for transfers between devices, exchange(): return lax.all_to_all(x, 'expert', 0, 0, tiled=True)  39 us
    ppermute x9, waiting for transfers between devices, shift(): lax.ppermute(x, 'tensor', [(i, (i + d) % members) for i in range(members)])  33.2 us
    ppermute x9, starting transfers between devices, shift(): lax.ppermute(x, 'tensor', [(i, (i + d) % members) for i in range(members)])  16.6 us
    pallas_call x3, Pallas kernels, combine(): pl.pallas_call(functools.partial(combine_kernel, order, len(others)), out...  10.5 us
    pallas_call x2, Pallas kernels, route(): pl.pallas_call(functools.partial(route_kernel, count, groups, members, ca...  6.88 us
    unnamed x38, local copies, waits for them, and re-layouts  6.22 us
  transfers between devices with their start and end apart: 14, of which 8 were waited for; matrix products, arithmetic and copies ran while one was open for 1% of the time, Pallas kernels for 28%

profile of v1, /device:TPU:4, one launch (start us, length us, event | category | flops | bytes accessed | tf_op | source)
XLA Modules:
  0.0 200.8 jit_solution(13816586728547466026)
XLA Ops:
  0.0 3.2 %collective-permute-start.1 = (bf16[128,2048]{1,0:T(8,128)(2,1)}, bf16[128,2048]{1,0:T(8,128)(2,1)S(1)}, u32[]{:S(2)}, u32[]{:S(2)}) collective-permute-start(bf16[128,2048]{1,0:T(8,128)(2,1)} %refs_5_.1), channel_id=1, source_target_pairs={{0,4},{2,6},{4,0},{6,2},{1,5},{3,7},{5,1},{7,3},{8,12},{10,14},{12... | collective-permute-start | bytes 1572872 | tf_op jit(solution)/shard_map/ppermute | solution.py:288
  3.2 0.7 convert_bitcast_fusion
  3.9 0.7 pad_maximum_fusion.refs_0_
  4.6 0.3 collective-permute-start
  4.9 10.6 %collective-permute-done.refs_1_ = f32[8,128]{1,0:T(8,128)S(1)} collective-permute-done((f32[8,128]{1,0:T(8,128)S(1)}, f32[8,128]{1,0:T(8,128)S(1)}, u32[]{:S(2)}, u32[]{:S(2)}) %collective-permute-start) | collective-permute-done | bytes 4128 | tf_op jit(solution)/shard_map/ppermute | solution.py:288
  15.5 0.6 copy-done.17
  16.1 0.8 copy-done.4
  16.9 3.5 %route.2 = (bf16[16,32,2048]{2,1,0:T(8,128)(2,1)}, bf16[2,256,128]{2,1,0:T(8,128)(2,1)}, bf16[2,256,128]{2,1,0:T(8,128)(2,1)}) custom-call(f32[8,128]{1,0:T(8,128)} %copy-done.13, f32[8,128]{1,0:T(8,128)} %copy-done.17, bf16[128,2048]{1,0:T(8,128)(2,1)} %refs_5_.1, bf16[128,2048]{1,0:T(8,128)(2,1)} %copy-done.4), custom_call_target="tpu_custom_call" | custom-call | flops 268435456 | bytes 3145728 | tf_op jit(solution)/shard_map/route/pallas_call | solution.py:87
  20.3 0.0 copy-start.3
  20.3 8.4 %all-to-all-start = ((bf16[16,32,2048]{2,1,0:T(8,128)(2,1)}), bf16[16,32,2048]{2,1,0:T(8,128)(2,1)S(1)}, u32[]{:S(2)}, u32[]{:S(2)}) async-start(bf16[16,32,2048]{2,1,0:T(8,128)(2,1)} %get-tuple-element.17), calls=%async_computation | async-start | bytes 4194304 | tf_op jit(solution)/shard_map/all_to_all | solution.py:291
  28.8 1.6 collective-permute-start.3
  30.4 1.7 collective-permute-start.2
  32.1 0.4 collective-permute-start.5
  32.5 2.9 %collective-permute-start.4 = (f32[8,128]{1,0:T(8,128)S(1)}, f32[8,128]{1,0:T(8,128)S(1)}, u32[]{:S(2)}, u32[]{:S(2)}) collective-permute-start(f32[8,128]{1,0:T(8,128)S(1)} %copy-done.14), channel_id=1, source_target_pairs={{0,6},{2,0},{4,2},{6,4},{1,7},{3,1},{5,3},{7,5},{8,14},{10,8},{12,... | collective-permute-start | bytes 12296 | tf_op jit(solution)/shard_map/ppermute | solution.py:288
  35.3 7.1 %collective-permute-done.5.refs_1_ = f32[8,128]{1,0:T(8,128)S(1)} collective-permute-done((f32[8,128]{1,0:T(8,128)S(1)}, f32[8,128]{1,0:T(8,128)S(1)}, u32[]{:S(2)}, u32[]{:S(2)}) %collective-permute-start.5) | collective-permute-done | bytes 4128 | tf_op jit(solution)/shard_map/ppermute | solution.py:288
  42.5 0.0 collective-permute-done.4.refs_0_
  42.5 0.5 copy-done.15
  43.0 0.0 copy-done.16
  43.1 0.2 copy-done.6
  43.3 0.8 copy-done.7
  44.1 3.4 %route.3 = (bf16[16,32,2048]{2,1,0:T(8,128)(2,1)}, bf16[2,256,128]{2,1,0:T(8,128)(2,1)}, bf16[2,256,128]{2,1,0:T(8,128)(2,1)}) custom-call(f32[8,128]{1,0:T(8,128)} %copy-done.16, f32[8,128]{1,0:T(8,128)} %copy-done.15, bf16[128,2048]{1,0:T(8,128)(2,1)} %copy-done.7, bf16[128,2048]{1,0:T(8,128)(2,1)} %copy-done.6), custom_call_target="tpu_custom_call" | custom-call | flops 268435456 | bytes 3145728 | tf_op jit(solution)/shard_map/route/pallas_call | solution.py:87
  47.6 6.8 %all-to-all-done = bf16[16,32,2048]{2,1,0:T(8,128)(2,1)S(1)} async-done(((bf16[16,32,2048]{2,1,0:T(8,128)(2,1)}), bf16[16,32,2048]{2,1,0:T(8,128)(2,1)S(1)}, u32[]{:S(2)}, u32[]{:S(2)}) %all-to-all-start) | async-done | bytes 2097184 | tf_op jit(solution)/shard_map/all_to_all | solution.py:291
  54.4 1.4 copy-done.5
  55.8 8.5 %all-to-all-start.2 = ((bf16[16,32,2048]{2,1,0:T(8,128)(2,1)}), bf16[16,32,2048]{2,1,0:T(8,128)(2,1)}, u32[]{:S(2)}, u32[]{:S(2)}) async-start(bf16[16,32,2048]{2,1,0:T(8,128)(2,1)} %get-tuple-element.21), calls=%async_computation.2 | async-start | bytes 4194304 | tf_op jit(solution)/shard_map/all_to_all | solution.py:291
  64.3 17.3 %shard_map.100 = (bf16[16,16,2048]{2,1,0:T(8,128)(2,1)}, bf16[16,16,2048]{2,1,0:T(8,128)(2,1)}) custom-call(bf16[512,2048]{1,0:T(8,128)(2,1)} %bitcast.10, bf16[2048,1408]{1,0:T(8,128)(2,1)} %bitcast.12, bf16[2048,1408]{1,0:T(8,128)(2,1)} %bitcast.14, bf16[1408,2048]{1,0:T(8,128)(2,1)} %bitcast.16), custom_call_target="tpu_custom_call" | custom-call | flops 8858370048 | bytes 21495808 | tf_op jit(solution)/shard_map/pallas_call | solution.py:197
  81.6 8.1 %all-to-all-done.2 = bf16[16,32,2048]{2,1,0:T(8,128)(2,1)} async-done(((bf16[16,32,2048]{2,1,0:T(8,128)(2,1)}), bf16[16,32,2048]{2,1,0:T(8,128)(2,1)}, u32[]{:S(2)}, u32[]{:S(2)}) %all-to-all-start.2) | async-done | bytes 2097184 | tf_op jit(solution)/shard_map/all_to_all | solution.py:291
  89.7 7.6 %all-to-all-start.4 = ((bf16[16,16,2048]{2,1,0:T(8,128)(2,1)}), bf16[16,16,2048]{2,1,0:T(8,128)(2,1)S(1)}, u32[]{:S(2)}, u32[]{:S(2)}) async-start(bf16[16,16,2048]{2,1,0:T(8,128)(2,1)} %get-tuple-element.24), calls=%async_computation.4 | async-start | bytes 2097152 | tf_op jit(solution)/shard_map/all_to_all | solution.py:291
  97.3 17.2 %shard_map.102 = bf16[16,32,2048]{2,1,0:T(8,128)(2,1)} custom-call(bf16[512,2048]{1,0:T(8,128)(2,1)} %bitcast.8.refs_0_, bf16[2048,1408]{1,0:T(8,128)(2,1)} %bitcast.13, bf16[2048,1408]{1,0:T(8,128)(2,1)} %bitcast.15, bf16[1408,2048]{1,0:T(8,128)(2,1)} %bitcast.17), custom_call_target="tpu_custom_call" | custom-call | flops 8858370048 | bytes 21495808 | tf_op jit(solution)/shard_map/pallas_call | solution.py:197
  114.6 0.0 copy-start.18
  114.6 1.0 copy-done.2
  115.6 7.3 %all-to-all-start.3 = ((bf16[16,32,2048]{2,1,0:T(8,128)(2,1)}), bf16[16,32,2048]{2,1,0:T(8,128)(2,1)S(1)}, u32[]{:S(2)}, u32[]{:S(2)}) async-start(bf16[16,32,2048]{2,1,0:T(8,128)(2,1)} %shard_map.102), calls=%async_computation.3 | async-start | bytes 4194304 | tf_op jit(solution)/shard_map/all_to_all | solution.py:291
  122.9 0.6 reshape.10.refs_3_
  123.5 0.7 fusion
  124.2 24.1 %all-to-all-done.3.refs_2_ = bf16[16,32,2048]{2,1,0:T(8,128)(2,1)S(1)} async-done(((bf16[16,32,2048]{2,1,0:T(8,128)(2,1)}), bf16[16,32,2048]{2,1,0:T(8,128)(2,1)S(1)}, u32[]{:S(2)}, u32[]{:S(2)}) %all-to-all-start.3) | async-done | bytes 2097184 | tf_op jit(solution)/shard_map/all_to_all | solution.py:291
  148.4 7.7 %all-to-all-start.1 = ((bf16[16,16,2048]{2,1,0:T(8,128)(2,1)}), bf16[16,16,2048]{2,1,0:T(8,128)(2,1)S(1)}, u32[]{:S(2)}, u32[]{:S(2)}) async-start(bf16[16,16,2048]{2,1,0:T(8,128)(2,1)} %get-tuple-element.18), calls=%async_computation.1 | async-start | bytes 2097152 | tf_op jit(solution)/shard_map/all_to_all | solution.py:291
  156.0 11.3 %shard_map.101.refs_4_ = bf16[4,128,2048]{2,1,0:T(8,128)(2,1)} custom-call(bf16[128,2048]{1,0:T(8,128)(2,1)} %refs_5_.1, bf16[128,2048]{1,0:T(8,128)(2,1)} %copy-done.7, bf16[128,2048]{1,0:T(8,128)(2,1)} %copy-done.4, bf16[128,2048]{1,0:T(8,128)(2,1)} %copy-done.6, bf16[704,2048]{1,0:T(8,128)(2,1)} %bitcast.18, bf16[704,2048]{1,0:T(8,128)(2,1)} %bitcast.19, ...), custom_call_target="tpu_custom_call" | custom-call | flops 4429185024 | bytes 12845056 | tf_op jit(solution)/shard_map/pallas_call | solution.py:197
  167.3 2.9 %shard_map.104 = bf16[128,2048]{1,0:T(8,128)(2,1)} custom-call(bf16[1,256,128]{2,1,0:T(8,128)(2,1)} %get-tuple-element.30.refs_0_, bf16[1,256,128]{2,1,0:T(8,128)(2,1)} %get-tuple-element.25.refs_1_, bf16[16,16,2048]{2,1,0:T(8,128)(2,1)} %copy-done.2, bf16[1,2048]{1,0:T(2,128)(2,1)} %reshape.10.refs_3_, bf16[4,128,2048]{2,1,0:T(8,128)(2,1)} %shard_map.101.refs_4_, ...), custom_call_target="tpu_custom_call" | custom-call | flops 268435456 | bytes 3145728 | tf_op jit(solution)/shard_map/pallas_call | solution.py:254
  170.3 3.3 %collective-permute-start.8 = (bf16[128,2048]{1,0:T(8,128)(2,1)}, bf16[128,2048]{1,0:T(8,128)(2,1)S(1)}, u32[]{:S(2)}, u32[]{:S(2)}) collective-permute-start(bf16[128,2048]{1,0:T(8,128)(2,1)} %shard_map.104), channel_id=1, source_target_pairs={{0,4},{2,6},{4,0},{6,2},{1,5},{3,7},{5,1},{7,3},{8,12},{10,14},{12... | collective-permute-start | bytes 1572872 | tf_op jit(solution)/shard_map/ppermute | solution.py:288
  173.5 4.0 %shard_map.103 = (bf16[128,2048]{1,0:T(8,128)(2,1)}, bf16[128,2048]{1,0:T(8,128)(2,1)}) custom-call(bf16[2,256,128]{2,1,0:T(8,128)(2,1)} %get-tuple-element.19.refs_0_, bf16[2,256,128]{2,1,0:T(8,128)(2,1)} %get-tuple-element.20.refs_1_, bf16[16,32,2048]{2,1,0:T(8,128)(2,1)} %copy-done, bf16[1,2048]{1,0:T(2,128)(2,1)} %reshape.10.refs_3_, ...), custom_call_target="tpu_custom_call" | custom-call | flops 268435456 | bytes 6291456 | tf_op jit(solution)/shard_map/pallas_call | solution.py:254
  177.5 0.7 collective-permute-start.6
  178.3 2.6 %collective-permute-start.7 = (bf16[128,2048]{1,0:T(8,128)(2,1)}, bf16[128,2048]{1,0:T(8,128)(2,1)S(1)}, u32[]{:S(2)}, u32[]{:S(2)}) collective-permute-start(bf16[128,2048]{1,0:T(8,128)(2,1)} %get-tuple-element.23), channel_id=1, source_target_pairs={{0,6},{2,0},{4,2},{6,4},{1,7},{3,1},{5,3},{7,5},{8,14},{10,8},{12,... | collective-permute-start | bytes 1572872 | tf_op jit(solution)/shard_map/ppermute | solution.py:288
  180.8 0.0 all-to-all-done.1.refs_2_
  180.8 6.1 %collective-permute-done.8.refs_8_ = bf16[128,2048]{1,0:T(8,128)(2,1)S(1)} collective-permute-done((bf16[128,2048]{1,0:T(8,128)(2,1)}, bf16[128,2048]{1,0:T(8,128)(2,1)S(1)}, u32[]{:S(2)}, u32[]{:S(2)}) %collective-permute-start.8) | collective-permute-done | bytes 524320 | tf_op jit(solution)/shard_map/ppermute | solution.py:288
  186.9 9.0 %collective-permute-done.6.refs_6_ = bf16[128,2048]{1,0:T(8,128)(2,1)S(1)} collective-permute-done((bf16[128,2048]{1,0:T(8,128)(2,1)}, bf16[128,2048]{1,0:T(8,128)(2,1)S(1)}, u32[]{:S(2)}, u32[]{:S(2)}) %collective-permute-start.6) | collective-permute-done | bytes 524320 | tf_op jit(solution)/shard_map/ppermute | solution.py:288
  195.9 0.4 collective-permute-done.7.refs_7_
  196.3 0.4 copy-done.9
  196.7 0.4 copy-done.10
  197.1 3.6 %shard_map.105 = bf16[128,2048]{1,0:T(8,128)(2,1)} custom-call(bf16[1,256,128]{2,1,0:T(8,128)(2,1)} %get-tuple-element.29.refs_0_, bf16[1,256,128]{2,1,0:T(8,128)(2,1)} %get-tuple-element.26.refs_1_, bf16[16,16,2048]{2,1,0:T(8,128)(2,1)} %copy-done.1, bf16[1,2048]{1,0:T(2,128)(2,1)} %reshape.10.refs_3_, bf16[4,128,2048]{2,1,0:T(8,128)(2,1)} %shard_map.101.refs_4_, ...), custom_call_target="tpu_custom_call" | custom-call | flops 268435456 | bytes 3145728 | tf_op jit(solution)/shard_map/pallas_call | solution.py:254
  (30 shorter events, 0.1 us)
Async XLA Ops:
  0.0 15.5 %collective-permute-start.1 = (bf16[128,2048]{1,0:T(8,128)(2,1)}, bf16[128,2048]{1,0:T(8,128)(2,1)S(1)}, u32[]{:S(2)}, u32[]{:S(2)}) collective-permute-start(bf16[128,2048]{1,0:T(8,128)(2,1)} %refs_5_.1), channel_id=1, source_target_pairs={{0,4},{2,6},{4,0},{6,2},{1,5},{3,7},{5,1},{7,3},{8,12},{10,14},{12... | collective-permute-start | bytes 1572872 | tf_op jit(solution)/shard_map/ppermute | solution.py:288
  4.6 10.9 %copy-start.13 = (f32[8,128]{1,0:T(8,128)}, f32[8,128]{1,0:T(8,128)S(1)}, u32[]{:S(2)}) copy-start(f32[8,128]{1,0:T(8,128)S(1)} %pad_maximum_fusion.refs_0_) | copy-start | bytes 12292
  4.6 10.9 %collective-permute-start = (f32[8,128]{1,0:T(8,128)S(1)}, f32[8,128]{1,0:T(8,128)S(1)}, u32[]{:S(2)}, u32[]{:S(2)}) collective-permute-start(f32[8,128]{1,0:T(8,128)S(1)} %pad_maximum_fusion.refs_0_), channel_id=1, source_target_pairs={{0,4},{2,6},{4,0},{6,2},{1,5},{3,7},{5,1},{7,3},{8,12},{10,14},{12... | collective-permute-start | bytes 12296 | tf_op jit(solution)/shard_map/ppermute | solution.py:288
  15.5 0.6 copy-start.17
  16.1 0.8 copy-start.4
  20.3 8.5 %copy-start.3 = (bf16[128,2048]{1,0:T(8,128)(2,1)S(1)}, bf16[128,2048]{1,0:T(8,128)(2,1)}, u32[]{:S(2)}) copy-start(bf16[128,2048]{1,0:T(8,128)(2,1)} %refs_5_.1) | copy-start | bytes 1572868
  20.3 11.8 %copy-start.14 = (f32[8,128]{1,0:T(8,128)S(1)}, f32[8,128]{1,0:T(8,128)}, u32[]{:S(2)}) copy-start(f32[8,128]{1,0:T(8,128)} %copy-done.13) | copy-start | bytes 12292
  20.3 34.1 %all-to-all-start = ((bf16[16,32,2048]{2,1,0:T(8,128)(2,1)}), bf16[16,32,2048]{2,1,0:T(8,128)(2,1)S(1)}, u32[]{:S(2)}, u32[]{:S(2)}) async-start(bf16[16,32,2048]{2,1,0:T(8,128)(2,1)} %get-tuple-element.17), calls=%async_computation | async-start | bytes 4194304 | tf_op jit(solution)/shard_map/all_to_all | solution.py:291
  28.8 13.7 %collective-permute-start.3 = (bf16[128,2048]{1,0:T(8,128)(2,1)S(1)}, bf16[128,2048]{1,0:T(8,128)(2,1)S(1)}, u32[]{:S(2)}, u32[]{:S(2)}) collective-permute-start(bf16[128,2048]{1,0:T(8,128)(2,1)S(1)} %copy-done.3), channel_id=1, source_target_pairs={{0,2},{2,4},{4,6},{6,0},{1,3},{3,5},{5,7},{7,1},{8,10},{10,12},{12... | collective-permute-start | bytes 1572872 | tf_op jit(solution)/shard_map/ppermute | solution.py:288
  30.4 12.1 %collective-permute-start.2 = (bf16[128,2048]{1,0:T(8,128)(2,1)S(1)}, bf16[128,2048]{1,0:T(8,128)(2,1)S(1)}, u32[]{:S(2)}, u32[]{:S(2)}) collective-permute-start(bf16[128,2048]{1,0:T(8,128)(2,1)S(1)} %copy-done.3), channel_id=1, source_target_pairs={{0,6},{2,0},{4,2},{6,4},{1,7},{3,1},{5,3},{7,5},{8,14},{10,8},{12,... | collective-permute-start | bytes 1572872 | tf_op jit(solution)/shard_map/ppermute | solution.py:288
  32.1 10.4 %collective-permute-start.5 = (f32[8,128]{1,0:T(8,128)S(1)}, f32[8,128]{1,0:T(8,128)S(1)}, u32[]{:S(2)}, u32[]{:S(2)}) collective-permute-start(f32[8,128]{1,0:T(8,128)S(1)} %copy-done.14), channel_id=1, source_target_pairs={{0,2},{2,4},{4,6},{6,0},{1,3},{3,5},{5,7},{7,1},{8,10},{10,12},{12... | collective-permute-start | bytes 12296 | tf_op jit(solution)/shard_map/ppermute | solution.py:288
  32.5 10.0 %collective-permute-start.4 = (f32[8,128]{1,0:T(8,128)S(1)}, f32[8,128]{1,0:T(8,128)S(1)}, u32[]{:S(2)}, u32[]{:S(2)}) collective-permute-start(f32[8,128]{1,0:T(8,128)S(1)} %copy-done.14), channel_id=1, source_target_pairs={{0,6},{2,0},{4,2},{6,4},{1,7},{3,1},{5,3},{7,5},{8,14},{10,8},{12,... | collective-permute-start | bytes 12296 | tf_op jit(solution)/shard_map/ppermute | solution.py:288
  42.5 0.6 copy-start.15
  42.5 0.6 copy-start.16
  42.5 0.8 copy-start.6
  43.3 0.8 copy-start.7
  54.4 1.4 copy-start.5
  55.8 33.9 %all-to-all-start.2 = ((bf16[16,32,2048]{2,1,0:T(8,128)(2,1)}), bf16[16,32,2048]{2,1,0:T(8,128)(2,1)}, u32[]{:S(2)}, u32[]{:S(2)}) async-start(bf16[16,32,2048]{2,1,0:T(8,128)(2,1)} %get-tuple-element.21), calls=%async_computation.2 | async-start | bytes 4194304 | tf_op jit(solution)/shard_map/all_to_all | solution.py:291
  89.7 24.9 %all-to-all-start.4 = ((bf16[16,16,2048]{2,1,0:T(8,128)(2,1)}), bf16[16,16,2048]{2,1,0:T(8,128)(2,1)S(1)}, u32[]{:S(2)}, u32[]{:S(2)}) async-start(bf16[16,16,2048]{2,1,0:T(8,128)(2,1)} %get-tuple-element.24), calls=%async_computation.4 | async-start | bytes 2097152 | tf_op jit(solution)/shard_map/all_to_all | solution.py:291
  114.6 8.3 %copy-start.18 = (bf16[2048]{0:T(1024)(128)(2,1)S(1)}, bf16[2048]{0:T(1024)(128)(2,1)}, u32[]{:S(2)}) copy-start(bf16[2048]{0:T(1024)(128)(2,1)} %param.19) | copy-start | bytes 12292
  114.6 8.9 %copy-start.11 = (bf16[2,256,128]{2,1,0:T(8,128)(2,1)S(1)}, bf16[2,256,128]{2,1,0:T(8,128)(2,1)}, u32[]{:S(2)}) copy-start(bf16[2,256,128]{2,1,0:T(8,128)(2,1)} %get-tuple-element.15) | copy-start | bytes 393220
  114.6 8.9 %copy-start.12 = (bf16[2,256,128]{2,1,0:T(8,128)(2,1)S(1)}, bf16[2,256,128]{2,1,0:T(8,128)(2,1)}, u32[]{:S(2)}) copy-start(bf16[2,256,128]{2,1,0:T(8,128)(2,1)} %get-tuple-element.16) | copy-start | bytes 393220
  114.6 1.0 copy-start.2
  115.6 32.7 %all-to-all-start.3 = ((bf16[16,32,2048]{2,1,0:T(8,128)(2,1)}), bf16[16,32,2048]{2,1,0:T(8,128)(2,1)S(1)}, u32[]{:S(2)}, u32[]{:S(2)}) async-start(bf16[16,32,2048]{2,1,0:T(8,128)(2,1)} %shard_map.102), calls=%async_computation.3 | async-start | bytes 4194304 | tf_op jit(solution)/shard_map/all_to_all | solution.py:291
  148.4 19.0 %copy-start = (bf16[16,32,2048]{2,1,0:T(8,128)(2,1)}, bf16[16,32,2048]{2,1,0:T(8,128)(2,1)S(1)}, u32[]{:S(2)}) copy-start(bf16[16,32,2048]{2,1,0:T(8,128)(2,1)S(1)} %all-to-all-done.3.refs_2_) | copy-start | bytes 6291460
  148.4 32.5 %all-to-all-start.1 = ((bf16[16,16,2048]{2,1,0:T(8,128)(2,1)}), bf16[16,16,2048]{2,1,0:T(8,128)(2,1)S(1)}, u32[]{:S(2)}, u32[]{:S(2)}) async-start(bf16[16,16,2048]{2,1,0:T(8,128)(2,1)} %get-tuple-element.18), calls=%async_computation.1 | async-start | bytes 2097152 | tf_op jit(solution)/shard_map/all_to_all | solution.py:291
  170.3 16.6 %collective-permute-start.8 = (bf16[128,2048]{1,0:T(8,128)(2,1)}, bf16[128,2048]{1,0:T(8,128)(2,1)S(1)}, u32[]{:S(2)}, u32[]{:S(2)}) collective-permute-start(bf16[128,2048]{1,0:T(8,128)(2,1)} %shard_map.104), channel_id=1, source_target_pairs={{0,4},{2,6},{4,0},{6,2},{1,5},{3,7},{5,1},{7,3},{8,12},{10,14},{12... | collective-permute-start | bytes 1572872 | tf_op jit(solution)/shard_map/ppermute | solution.py:288
  177.5 18.4 %collective-permute-start.6 = (bf16[128,2048]{1,0:T(8,128)(2,1)}, bf16[128,2048]{1,0:T(8,128)(2,1)S(1)}, u32[]{:S(2)}, u32[]{:S(2)}) collective-permute-start(bf16[128,2048]{1,0:T(8,128)(2,1)} %get-tuple-element.22), channel_id=1, source_target_pairs={{0,2},{2,4},{4,6},{6,0},{1,3},{3,5},{5,7},{7,1},{8,10},{10,12},{12... | collective-permute-start | bytes 1572872 | tf_op jit(solution)/shard_map/ppermute | solution.py:288
  178.3 18.0 %collective-permute-start.7 = (bf16[128,2048]{1,0:T(8,128)(2,1)}, bf16[128,2048]{1,0:T(8,128)(2,1)S(1)}, u32[]{:S(2)}, u32[]{:S(2)}) collective-permute-start(bf16[128,2048]{1,0:T(8,128)(2,1)} %get-tuple-element.23), channel_id=1, source_target_pairs={{0,6},{2,0},{4,2},{6,4},{1,7},{3,1},{5,3},{7,5},{8,14},{10,8},{12,... | collective-permute-start | bytes 1572872 | tf_op jit(solution)/shard_map/ppermute | solution.py:288
  180.8 15.4 %copy-start.1 = (bf16[16,16,2048]{2,1,0:T(8,128)(2,1)}, bf16[16,16,2048]{2,1,0:T(8,128)(2,1)S(1)}, u32[]{:S(2)}) copy-start(bf16[16,16,2048]{2,1,0:T(8,128)(2,1)S(1)} %all-to-all-done.1.refs_2_) | copy-start | bytes 3145732
  186.9 9.4 %copy-start.8 = (bf16[128,2048]{1,0:T(8,128)(2,1)}, bf16[128,2048]{1,0:T(8,128)(2,1)S(1)}, u32[]{:S(2)}) copy-start(bf16[128,2048]{1,0:T(8,128)(2,1)S(1)} %collective-permute-done.8.refs_8_) | copy-start | bytes 1572868
  195.9 0.8 copy-start.9
  196.3 0.8 copy-start.10
